TPU v7x, 128 devices: a whole 4x4x4 slice. The times are simulated.
128 devices in a mesh: dp: 8 (over y_hi, z), mp: 16 (over y_lo, x, core).
Axes of the slice: x: 4, y: 4 (y_hi: 2, y_lo: 2; y = y_hi * 2 + y_lo), z: 4, core: 2. Of those that a mesh axis runs over, the one named last changes fastest.
Arguments:
- weight: bfloat16 [5120, 32768], P('dp', 'mp'), may hold values from -0.078125 to 0.078125
- rank_map: int32 [16], replicated, may hold values from 0 to 15, each once
Outputs:
- quant_out: bfloat16 [5120, 32768], P(None, 'mp')
- scale_out: bfloat16 [5120, 256], P(None, 'mp')
- checksum: float32 [256], replicated
Inputs may be any that keep to these rules, and one draw needn't show every extreme that they name: `rank_map`: a permutation of 0 to 15.
All inputs are finite; a program needn't handle non-finite values.
Results may differ from a plain program's by a relative error of at most 0.0085.
Values may be sent and summed in bfloat16 or wider, within the bound.
A program may use at most 192 MiB of HBM per device.

v0:
```python
import math

import jax
import jax.numpy as jnp
from jax import lax
from jax.sharding import Mesh
from jax.sharding import PartitionSpec as P

D = 5120
MP = ("mp_0", "mp_1", "mp_2")
DP = ("dp_0", "dp_1")
DP_MP = ("dp_0", "dp_1", "mp_0", "mp_1", "mp_2")


floor_ratio = 0.25


def sent_together(arrays, axis, split_dim, concat_dim, along):
    widths = [math.prod(a.shape[along:]) for a in arrays]
    both = jnp.concatenate(
        [a.reshape(*a.shape[:along], w) for a, w in zip(arrays, widths)], axis=along
    )
    filled = lax.all_to_all(both, axis, split_axis=split_dim, concat_axis=concat_dim, tiled=True)
    pieces = jnp.split(filled, [sum(widths[:k]) for k in range(1, len(widths))], axis=along)
    return tuple(
        (b.reshape(*filled.shape[:along], *a.shape[along:]) for a, b in zip(arrays, pieces))
    )


def sent_together_2(arrays, axis, dim, along):
    widths = [a.shape[along] for a in arrays]
    both = jnp.concatenate(arrays, axis=along)
    filled = lax.all_gather(both, axis, axis=dim, tiled=True)
    return tuple(jnp.split(filled, [sum(widths[:k]) for k in range(1, len(widths))], axis=along))


def by_axis(shard, axes):
    for axis in axes:
        shard = lax.psum(shard, axis)
    return shard


def quantize(weight):
    rows, cols = weight.shape
    blocks = weight.astype(jnp.float32).reshape(rows, cols // 128, 128)
    peak = jnp.max(jnp.abs(blocks), axis=2)
    scale = (jnp.maximum(peak, floor_ratio / math.sqrt(D)) / 127.0).astype(jnp.bfloat16)
    quant = (blocks / scale.astype(jnp.float32)[:, :, None]).astype(jnp.bfloat16)
    return (quant.reshape(rows, cols), scale)


def inverse(rank_map):
    count = rank_map.shape[0]
    ids = jnp.arange(count)
    match = (rank_map[None, :] == ids[:, None]).astype(jnp.int32)
    return jnp.sum(ids[None, :] * match, axis=1)


def arrange(quant, scale, inv, count):
    rows, nblocks = scale.shape
    group = nblocks // count
    grouped = jnp.take(quant.reshape(rows, group, count, 128), inv, axis=2)
    scales = jnp.take(scale.reshape(rows, group, count), inv, axis=2)
    return (grouped, scales)


def settle(quant, scale):
    rows = quant.shape[0]
    return (quant.reshape(rows, -1), scale.reshape(rows, -1))


def local(weight, rank_map):
    count = lax.axis_size(MP)
    rank = lax.axis_index(MP)
    inv = inverse(rank_map)
    quant, scale = quantize(weight)
    grouped, scales = arrange(quant, scale, inv, count)
    moved_quant, moved_scale = sent_together((grouped, scales), MP, 2, 1, 3)
    local_quant, local_scale = settle(moved_quant, moved_scale)
    quant_out, scale_out = sent_together_2((local_quant, local_scale), DP, 0, 1)
    divisor = 127.0 * math.sqrt(D * 128)
    rows, nblocks = scale.shape
    partial_value = jnp.sum(quant.reshape(rows, nblocks, 128), axis=(0, 2), dtype=jnp.float32)
    whole = jnp.zeros((nblocks * count,), jnp.float32)
    whole = lax.dynamic_update_slice_in_dim(whole, partial_value, rank * nblocks, 0)
    totals = by_axis(whole, DP_MP)
    return (quant_out, scale_out, totals / divisor)


def solution(mesh):
    split = Mesh(mesh.devices.reshape(2, 4, 2, 4, 2), ("dp_0", "dp_1", "mp_0", "mp_1", "mp_2"))
    return jax.shard_map(
        local,
        mesh=split,
        in_specs=(P(DP, MP), P()),
        out_specs=(P(None, MP), P(None, MP), P()),
        check_vma=False,
    )
```

profile of v0, /device:TPU:0, one launch (start us, length us, event | category | flops | bytes accessed | tf_op | source)
XLA Modules:
  0.0 357.9 jit_solution(11573169486273010831)
XLA Ops:
  7.2 0.0 all-gather.2.cloned.1.call-start
  7.2 0.8 select_reduce_fusion
  8.0 3.1 copy.21
  11.2 0.5 bitcast_reduce_fusion
  11.7 0.6 gather_fusion.1
  12.3 2.1 copy.23
  14.4 3.2 copy.22
  17.6 5.6 %fusion.1 = bf16[640,16,128]{2,0,1:T(8,128)(2,1)} fusion(f32[640,1,16,128]{3,0,2,1:T(8,128)} %copy.22, f32[640,16]{0,1:T(8,128)S(1)} %get-tuple-element.18), kind=kLoop, calls=%fused_computation.11 | loop fusion | flops 2621440 | bytes 7905280 | tf_op jit(solution)/shard_map/convert_element_type | solution.py:48
  23.2 4.1 %gather_fusion = bf16[16,640,128]{2,1,0:T(8,128)(2,1)} fusion(bf16[640,16,128]{2,0,1:T(8,128)(2,1)} %fusion.1, s32[1024]{0:T(1024)S(1)} %pad_clamp_fusion), kind=kCustom, calls=%fused_computation | custom fusion | bytes 5242944 | tf_op jit(solution)/shard_map/jit(_take)/gather | solution.py:62
  27.3 0.0 copy-start
  27.3 2.2 broadcast_select_fusion
  29.5 0.3 copy-done
  29.8 0.3 bitcast_select_fusion
  30.1 3.5 pad_maximum_fusion
  33.6 6.2 %copy.24 = bf16[640,1,16,129]{0,3,1,2:T(8,128)(2,1)} copy(bf16[640,1,16,129]{3,0,2,1:T(8,128)(2,1)} %pad_maximum_fusion) | data formatting | bytes 5283840 | tf_op jit(solution)/shard_map/concatenate | solution.py:20
  39.9 40.4 %all_to_all.12 = bf16[640,1,16,129]{0,3,1,2:T(8,128)(2,1)S(1)} all-to-all(bf16[640,1,16,129]{0,3,1,2:T(8,128)(2,1)} %copy.24), channel_id=1, replica_groups=mesh['dp_0'=2,'dp_1'=4,'mp_0'=2,'mp_1'=4,'mp_2'=2] {'mp_0','mp_1','mp_2'}, dimensions={2} | all-to-all | bytes 5283840 | tf_op jit(solution)/shard_map/all_to_all | solution.py:23
  80.3 0.4 split.16
  80.6 1.7 pad_maximum_fusion.1
  82.4 0.0 all-gather.2.cloned.1.call-update
  82.4 0.6 convert_reduce_fusion
  83.0 0.1 bitcast_reduce_fusion.1
  83.1 0.2 dynamic_update_slice.3
  83.4 6.4 %psum.35 = f32[256]{0:T(256)S(1)} all-reduce(f32[256]{0:T(256)S(1)} %dynamic_update_slice.3), channel_id=1, replica_groups=mesh['dp_0'=2,'dp_1'=4,'mp_0'=2,'mp_1'=4,'mp_2'=2] {'dp_0'}, use_global_device_ids=true, to_apply=%region_4.5 | all-reduce | flops 256 | bytes 2048 | tf_op jit(solution)/shard_map/psum | solution.py:39
  89.8 11.9 %psum.36 = f32[256]{0:T(256)S(1)} all-reduce(f32[256]{0:T(256)S(1)} %psum.35), channel_id=1, replica_groups=mesh['dp_0'=2,'dp_1'=4,'mp_0'=2,'mp_1'=4,'mp_2'=2] {'dp_1'}, use_global_device_ids=true, to_apply=%region_5.6 | all-reduce | flops 256 | bytes 2048 | tf_op jit(solution)/shard_map/psum | solution.py:39
  101.7 5.1 %psum.37 = f32[256]{0:T(256)S(1)} all-reduce(f32[256]{0:T(256)S(1)} %psum.36), channel_id=1, replica_groups=mesh['dp_0'=2,'dp_1'=4,'mp_0'=2,'mp_1'=4,'mp_2'=2] {'mp_0'}, use_global_device_ids=true, to_apply=%region_6.7 | all-reduce | flops 256 | bytes 2048 | tf_op jit(solution)/shard_map/psum | solution.py:39
  106.9 8.6 %psum.38 = f32[256]{0:T(256)S(1)} all-reduce(f32[256]{0:T(256)S(1)} %psum.37), channel_id=1, replica_groups=mesh['dp_0'=2,'dp_1'=4,'mp_0'=2,'mp_1'=4,'mp_2'=2] {'mp_1'}, use_global_device_ids=true, to_apply=%region_7.8 | all-reduce | flops 256 | bytes 2048 | tf_op jit(solution)/shard_map/psum | solution.py:39
  115.5 2.5 psum.39
  117.9 0.6 broadcast_multiply_fusion
  118.5 185.4 %all-gather.2.cloned.1.call-done = bf16[5120,2064]{0,1:T(8,128)(2,1)} async-done(((bf16[640,2064]{0,1:T(8,128)(2,1)}), bf16[5120,2064]{0,1:T(8,128)(2,1)}) %all-gather.2.cloned.1.call-update) | async-done | bytes 21135376 | tf_op jit(solution)/shard_map/all_gather | solution.py:33
  303.9 17.3 %split.18 = bf16[5120,2048]{0,1:T(8,128)(2,1)} slice(bf16[5120,2064]{0,1:T(8,128)(2,1)} %all-gather.2.cloned.1.call-done), slice={[0:5120], [0:2048]} | slice | bytes 41943040 | tf_op jit(solution)/shard_map/split | solution.py:34
  321.2 28.2 %copy.25 = bf16[5120,2048]{1,0:T(8,128)(2,1)} copy(bf16[5120,2048]{0,1:T(8,128)(2,1)} %split.18) | data formatting | bytes 41943040
  349.4 1.6 split.19
  (7 shorter events, 0.1 us)
Async XLA Ops:
  7.2 296.7 %all-gather.2.cloned.1.call-start = ((), (), s32[]{:S(2)}) async-start(), calls=%async_computation.1 | async-start | bytes 23777280 | tf_op jit(solution)/shard_map/all_gather | solution.py:33
  27.3 2.5 copy-start
Sparse Core Ops, SparseCore 0:
  82.5 221.3 all-gather.1
where the time goes:
time: 359 us; the launch traced here: 358 us
  waiting for transfers between devices  185 us (52%)
  blocking collectives  74.9 us (21%)
  local copies, waits for them, and re-layouts  67.5 us (19%)
  other arithmetic  15.9 us (4%)
  between operations  14.1 us (4%)
    all_gather x1, waiting for transfers between devices, sent_together_2(): filled = lax.all_gather(both, axis, axis=dim, tiled=True)  185 us
    all_to_all x1, blocking collectives, sent_together(): lax.all_to_all(both, axis, split_axis=split_dim, concat_axis=concat_dim,...  40.4 us
    psum x5, blocking collectives, by_axis(): shard = lax.psum(shard, axis)  34.6 us
    unnamed x5, local copies, waits for them, and re-layouts  31.7 us
    split x2, local copies, waits for them, and re-layouts, sent_together_2(): jnp.split(filled, [sum(widths[:k]) for k in range(1, len(widths))], axis=...  18.9 us
  transfers between devices with their start and end apart: 1, of which 1 were waited for; matrix products, arithmetic and copies ran while one was open for 0% of the time, Pallas kernels for 0%

commit v1 on v0

v1 whole, which is shorter than its diff:
```python
import functools
import math

import jax
import jax.numpy as jnp
from jax import lax
from jax.experimental import pallas as pl
from jax.experimental.pallas import tpu as pltpu
from jax.sharding import PartitionSpec as P

MESH = pl.DeviceIdType.MESH
D = 5120
floor_ratio = 0.25
BLOCK = 128
ROWS = 640
PIECE = 656
N_MP = 16
N_DP = 8
GROUPS = 8
Z = 4
MIB = 1024 * 1024


def exchange(rank_ref, w_hbm, land, sums, w, staged, part, parts, w_sem, recv1, recvz, send, sem_a, sem_b, send_s):
    dp = lax.axis_index("dp")
    mp = lax.axis_index("mp")
    h, z = dp // Z, lax.rem(dp, Z)
    yl, x, c = mp // 8, lax.rem(mp // 2, 4), lax.rem(mp, 2)

    for q in range(N_MP):
        pltpu.make_async_copy(w_hbm.at[:, pl.ds(q * BLOCK, BLOCK)], w.at[q], w_sem).start()

    def z_at(dz):
        return lax.rem(z + dz, Z)

    def rank_at(yy, xx, cc):
        return yy * 8 + xx * 2 + cc

    def target(u, cc):
        return rank_at(lax.rem(yl + lax.rem(u, 2), 2), lax.rem(x + u // 2, 4), lax.rem(c + cc, 2))

    def origin(u, cs):
        return rank_at(lax.rem(yl + lax.rem(u, 2), 2), lax.rem(x + 4 - u // 2, 4), cs)

    barrier = pltpu.get_barrier_semaphore()

    def greet(n, _):
        hh, r = n // N_MP, lax.rem(mp + lax.rem(n, N_MP), N_MP)
        pl.semaphore_signal(barrier, inc=1, device_id=(lax.rem(h + hh, 2) * Z + z, r), device_id_type=MESH)
        return 0

    lax.fori_loop(1, 2 * N_MP, greet, 0)
    for dz in (1, 2, 3):
        for hh in (0, 1):
            pl.semaphore_signal(barrier, inc=1, device_id=(lax.rem(h + hh, 2) * Z + z_at(dz), mp), device_id_type=MESH)

    rows_i = lax.broadcasted_iota(jnp.int32, (BLOCK, BLOCK), 0)
    cols_i = lax.broadcasted_iota(jnp.int32, (BLOCK, BLOCK), 1)
    diag = rows_i == cols_i

    def quantize(r):
        j = jnp.int32(0)
        for q in range(N_MP):
            j = j + jnp.where(rank_ref[q] == r, jnp.int32(q), jnp.int32(0))
        j = jnp.minimum(j, N_MP - 1)
        acc = jnp.zeros((8, BLOCK), jnp.float32)
        scales = []
        for k in range(ROWS // BLOCK):
            blk = w[j, pl.ds(k * BLOCK, BLOCK), :].astype(jnp.float32)
            peak = jnp.max(jnp.abs(blk), axis=1, keepdims=True)
            scale = (jnp.maximum(peak, floor_ratio / math.sqrt(D)) / 127.0).astype(jnp.bfloat16).astype(jnp.float32)
            scale = jnp.broadcast_to(scale, (BLOCK, BLOCK))
            quant = (blk / scale).astype(jnp.bfloat16)
            staged[r, pl.ds(k * BLOCK, BLOCK), :] = quant
            acc = acc + jnp.sum(quant.astype(jnp.float32).reshape(BLOCK // 8, 8, BLOCK), axis=0)
            scales.append(jnp.sum(jnp.where(diag, scale, 0.0), axis=0, keepdims=True))
        scales.append(jnp.zeros((PIECE - ROWS - len(scales), BLOCK), jnp.float32))
        staged[r, pl.ds(ROWS, PIECE - ROWS), :] = jnp.concatenate(scales, axis=0).astype(jnp.bfloat16)
        part[pl.ds(r, 1), :] = jnp.sum(acc, axis=0, keepdims=True)

    def piece_copy(src, dst, sem_s, sem_r, dev):
        return pltpu.make_async_remote_copy(src, dst, sem_s, sem_r, device_id=dev, device_id_type=MESH)

    def first(u, own):
        for cc in (0, 1):
            r = target(u, cc)
            for hh in (0, 1):
                if own and cc == 0 and hh == 0:
                    continue
                dev = (lax.rem(h + hh, 2) * Z + z, r)
                piece_copy(staged.at[r], land.at[dp, mp], send.at[u], recv1.at[u, h * 2 + c], dev).start()

    def step_quant(u, _):
        quantize(target(u, 0))
        quantize(target(u, 1))
        return 0

    def await_recv(sem):
        piece_copy(staged.at[0], staged.at[0], send.at[0], sem, (dp, mp)).wait_recv()

    def spread(u, hs, cs, own=False):
        k = hs * 2 + cs
        if not own:
            await_recv(recv1.at[u, k])
        ref = land.at[hs * Z + z, origin(u, cs)]
        piece_copy(ref, ref, send.at[u], recvz.at[0, u, k], (h * Z + z_at(1), mp)).start()
        piece_copy(ref, ref, send.at[u], recvz.at[1, u, k], (h * Z + z_at(3), mp)).start()

    def onward(u):
        k = h
        await_recv(recvz.at[0, u, k])
        ref = land.at[z_at(3), origin(u, h)]
        piece_copy(ref, ref, send.at[u], recvz.at[2, u, k], (h * Z + z_at(1), mp)).start()
        k = 2 + h
        await_recv(recvz.at[1, u, k])
        ref = land.at[Z + z_at(1), origin(u, h)]
        piece_copy(ref, ref, send.at[u], recvz.at[2, u, k], (h * Z + z_at(3), mp)).start()

    def cross(u):
        for hs in (0, 1):
            k = hs * 2 + h
            await_recv(recvz.at[2, u, k])
            ref = land.at[hs * Z + z_at(2), origin(u, h)]
            piece_copy(ref, ref, send.at[u], recvz.at[2, u, k], ((1 - h) * Z + z, mp)).start()

    def spread_all(u):
        for cs in (h, 1 - h):
            for hs in (0, 1):
                spread(u, hs, cs)

    pltpu.make_async_copy(w, w, w_sem).wait()
    step_quant(0, 0)
    land[dp, mp, :, :] = staged[mp, :, :]
    pl.semaphore_wait(barrier, 2 * N_MP - 1 + 6)
    first(0, True)
    step_quant(1, 0)
    first(1, False)
    for cc in (0, 1):
        for hh in (0, 1):
            spread(0, lax.rem(h + hh, 2), lax.rem(c + cc, 2), own=(cc == 0 and hh == 0))

    def rest(u, _):
        step_quant(u, 0)
        first(u, False)
        return 0

    lax.fori_loop(2, GROUPS, rest, 0)

    parts[dp, :, :] = part[...]
    for hh in (0, 1):
        for dz in range(Z):
            if hh == 0 and dz == 0:
                continue
            dev = (lax.rem(h + hh, 2) * Z + z_at(dz), mp)
            piece_copy(part, parts.at[dp], send_s, sem_a, dev).start()

    spread_all(1)
    onward(0)

    def main(u, _):
        spread_all(u)
        onward(u - 1)
        cross(u - 2)
        return 0

    lax.fori_loop(2, GROUPS, main, 0)

    pltpu.make_async_copy(parts.at[pl.ds(0, 7)], parts.at[pl.ds(0, 7)], sem_a).wait()
    whole = jnp.sum(jnp.sum(parts[...], axis=0), axis=1, keepdims=True)
    sums[mp, :, :] = jnp.broadcast_to(whole, (N_MP, BLOCK))

    onward(GROUPS - 1)

    def share(n, _):
        dev = (dp, lax.rem(mp + n, N_MP))
        piece_copy(sums.at[mp], sums.at[mp], send_s, sem_b, dev).start()
        return 0

    lax.fori_loop(1, N_MP, share, 0)
    cross(GROUPS - 2)
    cross(GROUPS - 1)

    def finish(u, _):
        for k in (1 - h, 2, 3):
            await_recv(recvz.at[0, u, k])
        for k in (0, 1, 3 - h):
            await_recv(recvz.at[1, u, k])
        for k in (1 - h, 3 - h):
            await_recv(recvz.at[2, u, k])
        return 0

    lax.fori_loop(0, GROUPS, finish, 0)
    pltpu.make_async_copy(sums.at[pl.ds(0, 15)], sums.at[pl.ds(0, 15)], sem_b).wait()

    def sent(u, _):
        def one(n, _):
            piece_copy(staged.at[0], staged.at[0], send.at[u], w_sem, (dp, mp)).wait_send()
            return 0

        lax.fori_loop(0, jnp.where(u == 0, 15, 16), one, 0)
        return 0

    lax.fori_loop(0, GROUPS, sent, 0)

    def sent_small(n, _):
        piece_copy(part, part, send_s, w_sem, (dp, mp)).wait_send()
        return 0

    lax.fori_loop(0, 7 + 15, sent_small, 0)


def settle(rank_ref, land, sums, quant_out, scale_out, check_out, sem):
    for d in range(N_DP):
        for i in range(N_MP):
            pltpu.make_async_copy(
                land.at[d, i, pl.ds(0, ROWS), :],
                quant_out.at[pl.ds(d * ROWS, ROWS), pl.ds(i * BLOCK, BLOCK)],
                sem,
            ).start()
    n = PIECE - ROWS
    k_rows = ROWS // BLOCK
    out_i = lax.broadcasted_iota(jnp.int32, (k_rows * N_MP, N_MP * n), 0)
    in_i = lax.broadcasted_iota(jnp.int32, (k_rows * N_MP, N_MP * n), 1)
    pick = (in_i == lax.rem(out_i, N_MP) * n + out_i // N_MP).astype(jnp.bfloat16)
    eye = (
        lax.broadcasted_iota(jnp.int32, (BLOCK, BLOCK), 0) == lax.broadcasted_iota(jnp.int32, (BLOCK, BLOCK), 1)
    ).astype(jnp.bfloat16)

    def scales(d, _):
        rows = land[d, :, pl.ds(ROWS, n), :].reshape(N_MP * n, BLOCK)
        sorted_rows = jnp.dot(pick, rows, preferred_element_type=jnp.float32).astype(jnp.bfloat16)
        for k in range(k_rows):
            flat = lax.dot_general(
                eye, sorted_rows[k * N_MP : (k + 1) * N_MP], (((1,), (1,)), ((), ())), preferred_element_type=jnp.float32
            )
            scale_out[pl.ds(pl.multiple_of(d * ROWS + k * BLOCK, BLOCK), BLOCK), :] = flat.astype(jnp.bfloat16)
        return 0

    lax.fori_loop(0, N_DP, scales, 0)
    lane = lax.broadcasted_iota(jnp.int32, (N_MP, BLOCK), 1)
    total = jnp.zeros((N_MP, BLOCK), jnp.float32)
    for j in range(N_MP):
        total = total + jnp.where(lane == j, sums[:, rank_ref[j], :], 0.0)
    check_out[...] = total / (127.0 * math.sqrt(D * BLOCK))

    def done(n, _):
        pltpu.make_async_copy(
            land.at[0, 0, pl.ds(0, ROWS), :], quant_out.at[pl.ds(0, ROWS), pl.ds(0, BLOCK)], sem
        ).wait()
        return 0

    lax.fori_loop(0, N_DP * N_MP, done, 0)


def local(weight, rank_map):
    vmem = pl.BlockSpec(memory_space=pltpu.VMEM)
    smem = pl.BlockSpec(memory_space=pltpu.SMEM)
    hbm = pl.BlockSpec(memory_space=pl.ANY)
    dma = pltpu.SemaphoreType.DMA
    land, sums = pl.pallas_call(
        exchange,
        out_shape=(
            pltpu.VMEM((N_DP, N_MP, PIECE, BLOCK), jnp.bfloat16),
            pltpu.VMEM((N_MP, N_MP, BLOCK), jnp.float32),
        ),
        in_specs=[smem, pl.BlockSpec(memory_space=pltpu.HBM)],
        out_specs=(vmem, vmem),
        scratch_shapes=[
            pltpu.VMEM((N_MP, ROWS, BLOCK), jnp.bfloat16),
            pltpu.VMEM((N_MP, PIECE, BLOCK), jnp.bfloat16),
            pltpu.VMEM((N_MP, BLOCK), jnp.float32),
            pltpu.VMEM((N_DP, N_MP, BLOCK), jnp.float32),
            dma(()),
            dma((GROUPS, 4)),
            dma((3, GROUPS, 4)),
            dma((GROUPS,)),
            dma(()),
            dma(()),
            dma(()),
        ],
        compiler_params=pltpu.CompilerParams(collective_id=0, has_side_effects=True, vmem_limit_bytes=12 * MIB),
        name="exchange",
    )(rank_map, pltpu.with_memory_space_constraint(weight, pltpu.HBM))
    quant_out, scale_out, check = pl.pallas_call(
        settle,
        out_shape=(
            jax.ShapeDtypeStruct((D, N_MP * BLOCK), jnp.bfloat16),
            jax.ShapeDtypeStruct((D, N_MP), jnp.bfloat16),
            jax.ShapeDtypeStruct((N_MP, BLOCK), jnp.float32),
        ),
        in_specs=[smem, vmem, vmem],
        out_specs=(hbm, vmem, vmem),
        scratch_shapes=[dma(())],
        compiler_params=pltpu.CompilerParams(vmem_limit_bytes=12 * MIB),
        name="settle",
    )(rank_map, land, sums)
    return quant_out, scale_out, check[:, :N_MP].reshape(N_MP * N_MP)


def solution(mesh):
    return jax.shard_map(
        local,
        mesh=mesh,
        in_specs=(P("dp", "mp"), P()),
        out_specs=(P(None, "mp"), P(None, "mp"), P()),
        check_vma=False,
    )
```

time: 359 us -> 204 us (0.57)
  the two profiles are of different devices: /device:TPU:0 before, /device:TPU:31 now
where the time goes in v1:
time: 204 us
  Pallas kernels  201 us (99%)
  local copies, waits for them, and re-layouts  2.34 us (1%)
    pallas_call x1, Pallas kernels, local(): pl.pallas_call(exchange, out_shape=(pltpu.VMEM((N_DP, N_MP, PIECE, BLOCK)...  193 us
    pallas_call x1, Pallas kernels, local(): pl.pallas_call(settle, out_shape=(jax.ShapeDtypeStruct((D, N_MP * BLOCK),...  7.56 us

profile of v1, /device:TPU:31, one launch (start us, length us, event | category | flops | bytes accessed | tf_op | source)
XLA Modules:
  0.0 204.0 jit_solution(5316360630486903801)
XLA Ops:
  0.6 0.0 copy-start
  0.6 0.6 copy-done
  1.3 193.4 %exchange.1 = (bf16[8,16,656,128]{3,2,1,0:T(8,128)(2,1)S(1)}, f32[16,16,128]{2,1,0:T(8,128)S(1)}) custom-call(s32[16]{0:T(128)S(1)} %copy-done, bf16[640,2048]{1,0:T(8,128)(2,1)} %w_hbm.1), custom_call_target="tpu_custom_call" | custom-call | tf_op jit(solution)/shard_map/exchange/pallas_call | solution.py:260
  194.7 7.6 %settle.1 = (bf16[5120,2048]{1,0:T(8,128)(2,1)}, bf16[5120,16]{1,0:T(8,128)(2,1)S(1)}, f32[16,128]{1,0:T(8,128)S(1)}) custom-call(s32[16]{0:T(128)S(1)} %copy-done, bf16[8,16,656,128]{3,2,1,0:T(8,128)(2,1)S(1)} %get-tuple-element.8.land, f32[16,16,128]{2,1,0:T(8,128)S(1)} %get-tuple-element.9.sums), custom_call_target="tpu_custom_call" | custom-call | tf_op jit(solution)/shard_map/settle/pallas_call | solution.py:284
  202.3 0.6 reshape.9
  202.9 1.1 copy.5
Async XLA Ops:
  0.6 0.7 copy-start

commit v2 on v1

--- a/solution.py
+++ b/solution.py
@@ -16,16 +16,19 @@
 PIECE = 656
 N_MP = 16
 N_DP = 8
-GROUPS = 8
+STEPS = 8
 Z = 4
 MIB = 1024 * 1024
 
 
-def exchange(rank_ref, w_hbm, land, sums, w, staged, part, parts, w_sem, recv1, recvz, send, sem_a, sem_b, send_s):
+def exchange(
+    rank_ref, w_hbm, land, sums, w, staged, relay, part, parts, w_sem, recv1, recvr, recvz, send, send_x, sem_a, sem_b, send_s
+):
     dp = lax.axis_index("dp")
     mp = lax.axis_index("mp")
     h, z = dp // Z, lax.rem(dp, Z)
     yl, x, c = mp // 8, lax.rem(mp // 2, 4), lax.rem(mp, 2)
+    home = yl * 2 + h
 
     for q in range(N_MP):
         pltpu.make_async_copy(w_hbm.at[:, pl.ds(q * BLOCK, BLOCK)], w.at[q], w_sem).start()
@@ -36,23 +39,31 @@
     def rank_at(yy, xx, cc):
         return yy * 8 + xx * 2 + cc
 
-    def target(u, cc):
-        return rank_at(lax.rem(yl + lax.rem(u, 2), 2), lax.rem(x + u // 2, 4), lax.rem(c + cc, 2))
-
-    def origin(u, cs):
-        return rank_at(lax.rem(yl + lax.rem(u, 2), 2), lax.rem(x + 4 - u // 2, 4), cs)
+    def shift(m):
+        return m + m // 2 - 2 * (m // 3)
+
+    def target(m, yy, cc):
+        return rank_at(yy, lax.rem(x + shift(m), 4), cc)
+
+    def origin(s, yy):
+        return rank_at(yy, lax.rem(x + 4 - shift(s // 2), 4), lax.rem(c + s, 2))
 
     barrier = pltpu.get_barrier_semaphore()
 
-    def greet(n, _):
-        hh, r = n // N_MP, lax.rem(mp + lax.rem(n, N_MP), N_MP)
-        pl.semaphore_signal(barrier, inc=1, device_id=(lax.rem(h + hh, 2) * Z + z, r), device_id_type=MESH)
-        return 0
-
-    lax.fori_loop(1, 2 * N_MP, greet, 0)
-    for dz in (1, 2, 3):
-        for hh in (0, 1):
-            pl.semaphore_signal(barrier, inc=1, device_id=(lax.rem(h + hh, 2) * Z + z_at(dz), mp), device_id_type=MESH)
+    def greet(dev):
+        pl.semaphore_signal(barrier, inc=1, device_id=dev, device_id_type=MESH)
+
+    def greet_mp(n, _):
+        greet((dp, lax.rem(mp + n, N_MP)))
+        return 0
+
+    def greet_dp(n, _):
+        greet((lax.rem(dp + n, N_DP), mp))
+        return 0
+
+    lax.fori_loop(1, N_MP, greet_mp, 0)
+    lax.fori_loop(1, N_DP, greet_dp, 0)
+    greet(((1 - h) * Z + z, rank_at(1 - yl, x, c)))
 
     rows_i = lax.broadcasted_iota(jnp.int32, (BLOCK, BLOCK), 0)
     cols_i = lax.broadcasted_iota(jnp.int32, (BLOCK, BLOCK), 1)
@@ -78,98 +89,114 @@
         staged[r, pl.ds(ROWS, PIECE - ROWS), :] = jnp.concatenate(scales, axis=0).astype(jnp.bfloat16)
         part[pl.ds(r, 1), :] = jnp.sum(acc, axis=0, keepdims=True)
 
+    def quantize_step(m):
+        def one(n, _):
+            quantize(target(m, n // 2, lax.rem(n, 2)))
+            return 0
+
+        lax.fori_loop(0, 4, one, 0)
+
     def piece_copy(src, dst, sem_s, sem_r, dev):
         return pltpu.make_async_remote_copy(src, dst, sem_s, sem_r, device_id=dev, device_id_type=MESH)
 
-    def first(u, own):
-        for cc in (0, 1):
-            r = target(u, cc)
-            for hh in (0, 1):
-                if own and cc == 0 and hh == 0:
-                    continue
-                dev = (lax.rem(h + hh, 2) * Z + z, r)
-                piece_copy(staged.at[r], land.at[dp, mp], send.at[u], recv1.at[u, h * 2 + c], dev).start()
-
-    def step_quant(u, _):
-        quantize(target(u, 0))
-        quantize(target(u, 1))
-        return 0
-
     def await_recv(sem):
-        piece_copy(staged.at[0], staged.at[0], send.at[0], sem, (dp, mp)).wait_recv()
-
-    def spread(u, hs, cs, own=False):
-        k = hs * 2 + cs
+        piece_copy(staged.at[0], staged.at[0], send_x, sem, (dp, mp)).wait_recv()
+
+    def along_x(m, cores):
+        for cc in cores:
+            to = lax.rem(c + cc, 2)
+            s = 2 * m + cc
+            dev = (dp, target(m, yl, to))
+            piece_copy(staged.at[target(m, yl, to)], land.at[dp, mp], send_x, recv1.at[s, home], dev).start()
+            piece_copy(staged.at[target(m, 1 - yl, to)], relay.at[s], send_x, recvr.at[s], dev).start()
+
+    def spread(s, k):
+        ref = land.at[lax.rem(k, 2) * Z + z, origin(s, k // 2)]
+        piece_copy(ref, ref, send.at[s], recvz.at[0, s, k], (h * Z + z_at(1), mp)).start()
+        piece_copy(ref, ref, send.at[s], recvz.at[1, s, k], (h * Z + z_at(3), mp)).start()
+
+    def along_y(s, own=False):
+        i = origin(s, yl)
         if not own:
-            await_recv(recv1.at[u, k])
-        ref = land.at[hs * Z + z, origin(u, cs)]
-        piece_copy(ref, ref, send.at[u], recvz.at[0, u, k], (h * Z + z_at(1), mp)).start()
-        piece_copy(ref, ref, send.at[u], recvz.at[1, u, k], (h * Z + z_at(3), mp)).start()
-
-    def onward(u):
-        k = h
-        await_recv(recvz.at[0, u, k])
-        ref = land.at[z_at(3), origin(u, h)]
-        piece_copy(ref, ref, send.at[u], recvz.at[2, u, k], (h * Z + z_at(1), mp)).start()
-        k = 2 + h
-        await_recv(recvz.at[1, u, k])
-        ref = land.at[Z + z_at(1), origin(u, h)]
-        piece_copy(ref, ref, send.at[u], recvz.at[2, u, k], (h * Z + z_at(3), mp)).start()
-
-    def cross(u):
+            await_recv(recv1.at[s, home])
+        ref = land.at[dp, i]
+        piece_copy(ref, ref, send.at[s], recv1.at[s, home], ((1 - h) * Z + z, mp)).start()
+        if not own:
+            await_recv(recvr.at[s])
+        ref = staged.at[rank_at(1 - yl, x, c)] if own else relay.at[s]
+        for hh in (0, 1):
+            dev = (lax.rem(h + hh, 2) * Z + z, rank_at(1 - yl, x, c))
+            piece_copy(ref, land.at[dp, i], send.at[s], recv1.at[s, home], dev).start()
+        spread(s, home)
+
+    def spread_rest(s):
+        for k in (yl * 2 + 1 - h, (1 - yl) * 2 + h, (1 - yl) * 2 + 1 - h):
+            await_recv(recv1.at[s, k])
+            spread(s, k)
+
+    def onward(s):
+        k = h * 2
+        await_recv(recvz.at[0, s, k])
+        ref = land.at[z_at(3), origin(s, h)]
+        piece_copy(ref, ref, send.at[s], recvz.at[2, s, k], (h * Z + z_at(1), mp)).start()
+        k = h * 2 + 1
+        await_recv(recvz.at[1, s, k])
+        ref = land.at[Z + z_at(1), origin(s, h)]
+        piece_copy(ref, ref, send.at[s], recvz.at[2, s, k], (h * Z + z_at(3), mp)).start()
+
+    def cross(s):
         for hs in (0, 1):
-            k = hs * 2 + h
-            await_recv(recvz.at[2, u, k])
-            ref = land.at[hs * Z + z_at(2), origin(u, h)]
-            piece_copy(ref, ref, send.at[u], recvz.at[2, u, k], ((1 - h) * Z + z, mp)).start()
-
-    def spread_all(u):
-        for cs in (h, 1 - h):
-            for hs in (0, 1):
-                spread(u, hs, cs)
+            k = h * 2 + hs
+            await_recv(recvz.at[2, s, k])
+            ref = land.at[hs * Z + z_at(2), origin(s, h)]
+            piece_copy(ref, ref, send.at[s], recvz.at[2, s, k], ((1 - h) * Z + z, mp)).start()
 
     pltpu.make_async_copy(w, w, w_sem).wait()
-    step_quant(0, 0)
+    quantize_step(0)
     land[dp, mp, :, :] = staged[mp, :, :]
-    pl.semaphore_wait(barrier, 2 * N_MP - 1 + 6)
-    first(0, True)
-    step_quant(1, 0)
-    first(1, False)
-    for cc in (0, 1):
-        for hh in (0, 1):
-            spread(0, lax.rem(h + hh, 2), lax.rem(c + cc, 2), own=(cc == 0 and hh == 0))
-
-    def rest(u, _):
-        step_quant(u, 0)
-        first(u, False)
-        return 0
-
-    lax.fori_loop(2, GROUPS, rest, 0)
+    pl.semaphore_wait(barrier, N_MP + N_DP - 1)
+    along_x(0, (1,))
+    along_y(0, own=True)
+
+    def rest(m, _):
+        quantize_step(m)
+        along_x(m, (0, 1))
+        return 0
+
+    lax.fori_loop(1, 2, rest, 0)
+    along_y(1)
+    spread_rest(0)
+    lax.fori_loop(2, 4, rest, 0)
 
     parts[dp, :, :] = part[...]
-    for hh in (0, 1):
-        for dz in range(Z):
-            if hh == 0 and dz == 0:
-                continue
-            dev = (lax.rem(h + hh, 2) * Z + z_at(dz), mp)
-            piece_copy(part, parts.at[dp], send_s, sem_a, dev).start()
-
-    spread_all(1)
+
+    def give(n, _):
+        dev = (lax.rem(dp + n, N_DP), mp)
+        piece_copy(part, parts.at[dp], send_s, sem_a, dev).start()
+        return 0
+
+    lax.fori_loop(1, N_DP, give, 0)
+
+    along_y(2)
+    spread_rest(1)
     onward(0)
 
-    def main(u, _):
-        spread_all(u)
-        onward(u - 1)
-        cross(u - 2)
-        return 0
-
-    lax.fori_loop(2, GROUPS, main, 0)
+    def main(s, _):
+        along_y(s + 1)
+        spread_rest(s)
+        onward(s - 1)
+        cross(s - 2)
+        return 0
+
+    lax.fori_loop(2, STEPS - 1, main, 0)
+    spread_rest(STEPS - 1)
 
     pltpu.make_async_copy(parts.at[pl.ds(0, 7)], parts.at[pl.ds(0, 7)], sem_a).wait()
     whole = jnp.sum(jnp.sum(parts[...], axis=0), axis=1, keepdims=True)
     sums[mp, :, :] = jnp.broadcast_to(whole, (N_MP, BLOCK))
 
-    onward(GROUPS - 1)
+    onward(STEPS - 2)
+    cross(STEPS - 3)
 
     def share(n, _):
         dev = (dp, lax.rem(mp + n, N_MP))
@@ -177,30 +204,37 @@
         return 0
 
     lax.fori_loop(1, N_MP, share, 0)
-    cross(GROUPS - 2)
-    cross(GROUPS - 1)
-
-    def finish(u, _):
-        for k in (1 - h, 2, 3):
-            await_recv(recvz.at[0, u, k])
-        for k in (0, 1, 3 - h):
-            await_recv(recvz.at[1, u, k])
-        for k in (1 - h, 3 - h):
-            await_recv(recvz.at[2, u, k])
-        return 0
-
-    lax.fori_loop(0, GROUPS, finish, 0)
+    onward(STEPS - 1)
+    cross(STEPS - 2)
+    cross(STEPS - 1)
+
+    def finish(s, _):
+        for k in (1, 2, 3):
+            await_recv(recvz.at[0, s, lax.rem(h * 2 + k, 4)])
+        for k in (1, 2, 3):
+            await_recv(recvz.at[1, s, lax.rem(h * 2 + 1 + k, 4)])
+        for k in (0, 1):
+            await_recv(recvz.at[2, s, (1 - h) * 2 + k])
+        return 0
+
+    lax.fori_loop(0, STEPS, finish, 0)
     pltpu.make_async_copy(sums.at[pl.ds(0, 15)], sums.at[pl.ds(0, 15)], sem_b).wait()
 
-    def sent(u, _):
+    def sent(s, _):
         def one(n, _):
-            piece_copy(staged.at[0], staged.at[0], send.at[u], w_sem, (dp, mp)).wait_send()
+            piece_copy(staged.at[0], staged.at[0], send.at[s], w_sem, (dp, mp)).wait_send()
             return 0
 
-        lax.fori_loop(0, jnp.where(u == 0, 15, 16), one, 0)
-        return 0
-
-    lax.fori_loop(0, GROUPS, sent, 0)
+        lax.fori_loop(0, 15, one, 0)
+        return 0
+
+    lax.fori_loop(0, STEPS, sent, 0)
+
+    def sent_x(n, _):
+        piece_copy(staged.at[0], staged.at[0], send_x, w_sem, (dp, mp)).wait_send()
+        return 0
+
+    lax.fori_loop(0, 14, sent_x, 0)
 
     def sent_small(n, _):
         piece_copy(part, part, send_s, w_sem, (dp, mp)).wait_send()
@@ -268,12 +302,15 @@
         scratch_shapes=[
             pltpu.VMEM((N_MP, ROWS, BLOCK), jnp.bfloat16),
             pltpu.VMEM((N_MP, PIECE, BLOCK), jnp.bfloat16),
+            pltpu.VMEM((STEPS, PIECE, BLOCK), jnp.bfloat16),
             pltpu.VMEM((N_MP, BLOCK), jnp.float32),
             pltpu.VMEM((N_DP, N_MP, BLOCK), jnp.float32),
             dma(()),
-            dma((GROUPS, 4)),
-            dma((3, GROUPS, 4)),
-            dma((GROUPS,)),
+            dma((STEPS, 4)),
+            dma((STEPS,)),
+            dma((3, STEPS, 4)),
+            dma((STEPS,)),
+            dma(()),
             dma(()),
             dma(()),
             dma(()),

time: 204 us -> 182 us (0.89)
  the two profiles are of different devices: /device:TPU:31 before, /device:TPU:0 now
where the time goes in v2:
time: 182 us; the launch traced here: 181 us
  Pallas kernels  178 us (98%)
  local copies, waits for them, and re-layouts  2.34 us (1%)
    pallas_call x1, Pallas kernels, local(): pl.pallas_call(exchange, out_shape=(pltpu.VMEM((N_DP, N_MP, PIECE, BLOCK)...  171 us
    pallas_call x1, Pallas kernels, local(): pl.pallas_call(settle, out_shape=(jax.ShapeDtypeStruct((D, N_MP * BLOCK),...  7.56 us

profile of v2, /device:TPU:0, one launch (start us, length us, event | category | flops | bytes accessed | tf_op | source)
XLA Modules:
  0.0 181.4 jit_solution(2420860783628648083)
XLA Ops:
  0.6 0.0 copy-start
  0.6 0.6 copy-done
  1.3 170.9 %exchange.1 = (bf16[8,16,656,128]{3,2,1,0:T(8,128)(2,1)S(1)}, f32[16,16,128]{2,1,0:T(8,128)S(1)}) custom-call(s32[16]{0:T(128)S(1)} %copy-done, bf16[640,2048]{1,0:T(8,128)(2,1)} %w_hbm.1), custom_call_target="tpu_custom_call" | custom-call | tf_op jit(solution)/shard_map/exchange/pallas_call | solution.py:294
  172.2 7.6 %settle.1 = (bf16[5120,2048]{1,0:T(8,128)(2,1)}, bf16[5120,16]{1,0:T(8,128)(2,1)S(1)}, f32[16,128]{1,0:T(8,128)S(1)}) custom-call(s32[16]{0:T(128)S(1)} %copy-done, bf16[8,16,656,128]{3,2,1,0:T(8,128)(2,1)S(1)} %get-tuple-element.8.land, f32[16,16,128]{2,1,0:T(8,128)S(1)} %get-tuple-element.9.sums), custom_call_target="tpu_custom_call" | custom-call | tf_op jit(solution)/shard_map/settle/pallas_call | solution.py:321
  179.7 0.6 reshape.9
  180.4 1.1 copy.5
Async XLA Ops:
  0.6 0.7 copy-start

commit v3 on v2

--- a/solution.py
+++ b/solution.py
@@ -13,7 +13,7 @@
 floor_ratio = 0.25
 BLOCK = 128
 ROWS = 640
-PIECE = 656
+PIECE = 648
 N_MP = 16
 N_DP = 8
 STEPS = 8
@@ -22,7 +22,7 @@
 
 
 def exchange(
-    rank_ref, w_hbm, land, sums, w, staged, relay, part, parts, w_sem, recv1, recvr, recvz, send, send_x, sem_a, sem_b, send_s
+    rank_hbm, w_hbm, land, sums, rank_ref, w, staged, relay, part, parts, rank_sem, w_sem, recv1, recvr, recvz, send, send_x, sem_a, sem_b, send_s
 ):
     dp = lax.axis_index("dp")
     mp = lax.axis_index("mp")
@@ -30,6 +30,7 @@
     yl, x, c = mp // 8, lax.rem(mp // 2, 4), lax.rem(mp, 2)
     home = yl * 2 + h
 
+    pltpu.make_async_copy(rank_hbm, rank_ref, rank_sem).start()
     for q in range(N_MP):
         pltpu.make_async_copy(w_hbm.at[:, pl.ds(q * BLOCK, BLOCK)], w.at[q], w_sem).start()
 
@@ -96,6 +97,9 @@
 
         lax.fori_loop(0, 4, one, 0)
 
+    def thin(s, way):
+        return jnp.logical_or(s == 1 + way, s == 3 + way)
+
     def piece_copy(src, dst, sem_s, sem_r, dev):
         return pltpu.make_async_remote_copy(src, dst, sem_s, sem_r, device_id=dev, device_id_type=MESH)
 
@@ -112,51 +116,77 @@
 
     def spread(s, k):
         ref = land.at[lax.rem(k, 2) * Z + z, origin(s, k // 2)]
-        piece_copy(ref, ref, send.at[s], recvz.at[0, s, k], (h * Z + z_at(1), mp)).start()
-        piece_copy(ref, ref, send.at[s], recvz.at[1, s, k], (h * Z + z_at(3), mp)).start()
-
-    def along_y(s, own=False):
-        i = origin(s, yl)
+        for way, dz in ((0, 1), (1, 3)):
+
+            @pl.when(jnp.logical_or(k // 2 == h, jnp.logical_not(thin(s, way))))
+            def _():
+                piece_copy(ref, ref, send.at[s], recvz.at[way, s, k], (h * Z + z_at(dz), mp)).start()
+
+    def over_y(s, own=False):
         if not own:
             await_recv(recv1.at[s, home])
-        ref = land.at[dp, i]
+        ref = land.at[dp, origin(s, yl)]
         piece_copy(ref, ref, send.at[s], recv1.at[s, home], ((1 - h) * Z + z, mp)).start()
+        spread(s, home)
+
+    def beside_y(s, own=False):
         if not own:
             await_recv(recvr.at[s])
         ref = staged.at[rank_at(1 - yl, x, c)] if own else relay.at[s]
         for hh in (0, 1):
             dev = (lax.rem(h + hh, 2) * Z + z, rank_at(1 - yl, x, c))
-            piece_copy(ref, land.at[dp, i], send.at[s], recv1.at[s, home], dev).start()
-        spread(s, home)
+            piece_copy(ref, land.at[dp, origin(s, yl)], send.at[s], recv1.at[s, home], dev).start()
+
+    def along_y(s):
+        over_y(s)
+        beside_y(s)
 
     def spread_rest(s):
         for k in (yl * 2 + 1 - h, (1 - yl) * 2 + h, (1 - yl) * 2 + 1 - h):
             await_recv(recv1.at[s, k])
             spread(s, k)
 
-    def onward(s):
-        k = h * 2
-        await_recv(recvz.at[0, s, k])
-        ref = land.at[z_at(3), origin(s, h)]
-        piece_copy(ref, ref, send.at[s], recvz.at[2, s, k], (h * Z + z_at(1), mp)).start()
-        k = h * 2 + 1
-        await_recv(recvz.at[1, s, k])
-        ref = land.at[Z + z_at(1), origin(s, h)]
-        piece_copy(ref, ref, send.at[s], recvz.at[2, s, k], (h * Z + z_at(3), mp)).start()
+    def arrived(way, s, k):
+        block = z_at(2) if way == 2 else (z_at(3) if way == 0 else z_at(1))
+        return land.at[lax.rem(k, 2) * Z + block, origin(s, k // 2)]
+
+    def onward(s, rows=(0,)):
+        for row in rows:
+            for way, dz in ((0, 1), (1, 3)):
+                k = lax.rem(h + row, 2) * 2 + way
+                await_recv(recvz.at[way, s, k])
+                ref = arrived(way, s, k)
+                piece_copy(ref, ref, send.at[s], recvz.at[2, s, k], (h * Z + z_at(dz), mp)).start()
+
+    def over(way, s, k):
+        ref = arrived(way, s, k)
+        piece_copy(ref, ref, send.at[s], recvz.at[way, s, k], ((1 - h) * Z + z, mp)).start()
+
+    def cross_near(s):
+        for way in (0, 1):
+
+            @pl.when(thin(s, way))
+            def _():
+                over(way, s, h * 2 + way)
+                await_recv(recvz.at[way, s, h * 2 + 1 - way])
+                over(way, s, h * 2 + 1 - way)
 
     def cross(s):
         for hs in (0, 1):
-            k = h * 2 + hs
-            await_recv(recvz.at[2, s, k])
-            ref = land.at[hs * Z + z_at(2), origin(s, h)]
-            piece_copy(ref, ref, send.at[s], recvz.at[2, s, k], ((1 - h) * Z + z, mp)).start()
-
+            await_recv(recvz.at[2, s, h * 2 + hs])
+            over(2, s, h * 2 + hs)
+
+    pltpu.make_async_copy(rank_hbm, rank_ref, rank_sem).wait()
     pltpu.make_async_copy(w, w, w_sem).wait()
-    quantize_step(0)
+    quantize(mp)
     land[dp, mp, :, :] = staged[mp, :, :]
     pl.semaphore_wait(barrier, N_MP + N_DP - 1)
+    over_y(0, own=True)
+    quantize(target(0, 1 - yl, c))
+    beside_y(0, own=True)
+    quantize(target(0, yl, 1 - c))
+    quantize(target(0, 1 - yl, 1 - c))
     along_x(0, (1,))
-    along_y(0, own=True)
 
     def rest(m, _):
         quantize_step(m)
@@ -185,6 +215,7 @@
         along_y(s + 1)
         spread_rest(s)
         onward(s - 1)
+        cross_near(s - 1)
         cross(s - 2)
         return 0
 
@@ -204,20 +235,27 @@
         return 0
 
     lax.fori_loop(1, N_MP, share, 0)
-    onward(STEPS - 1)
+    onward(STEPS - 1, rows=(0, 1))
     cross(STEPS - 2)
-    cross(STEPS - 1)
 
     def finish(s, _):
-        for k in (1, 2, 3):
-            await_recv(recvz.at[0, s, lax.rem(h * 2 + k, 4)])
-        for k in (1, 2, 3):
-            await_recv(recvz.at[1, s, lax.rem(h * 2 + 1 + k, 4)])
-        for k in (0, 1):
-            await_recv(recvz.at[2, s, (1 - h) * 2 + k])
+        for way in (0, 1):
+
+            @pl.when(jnp.logical_not(thin(s, way)))
+            def _():
+                await_recv(recvz.at[way, s, h * 2 + 1 - way])
+
+            @pl.when(s < STEPS - 1)
+            def _():
+                await_recv(recvz.at[way, s, (1 - h) * 2 + way])
+
+            await_recv(recvz.at[way, s, (1 - h) * 2 + 1 - way])
+            await_recv(recvz.at[2, s, (1 - h) * 2 + way])
         return 0
 
     lax.fori_loop(0, STEPS, finish, 0)
+    await_recv(recvz.at[2, STEPS - 1, h * 2])
+    await_recv(recvz.at[2, STEPS - 1, h * 2 + 1])
     pltpu.make_async_copy(sums.at[pl.ds(0, 15)], sums.at[pl.ds(0, 15)], sem_b).wait()
 
     def sent(s, _):
@@ -243,7 +281,8 @@
     lax.fori_loop(0, 7 + 15, sent_small, 0)
 
 
-def settle(rank_ref, land, sums, quant_out, scale_out, check_out, sem):
+def settle(rank_hbm, land, sums, quant_out, scale_out, check_out, rank_ref, rank_sem, sem):
+    pltpu.make_async_copy(rank_hbm, rank_ref, rank_sem).start()
     for d in range(N_DP):
         for i in range(N_MP):
             pltpu.make_async_copy(
@@ -256,26 +295,22 @@
     out_i = lax.broadcasted_iota(jnp.int32, (k_rows * N_MP, N_MP * n), 0)
     in_i = lax.broadcasted_iota(jnp.int32, (k_rows * N_MP, N_MP * n), 1)
     pick = (in_i == lax.rem(out_i, N_MP) * n + out_i // N_MP).astype(jnp.bfloat16)
-    eye = (
-        lax.broadcasted_iota(jnp.int32, (BLOCK, BLOCK), 0) == lax.broadcasted_iota(jnp.int32, (BLOCK, BLOCK), 1)
-    ).astype(jnp.bfloat16)
-
-    def scales(d, _):
+
+    for d in range(N_DP):
         rows = land[d, :, pl.ds(ROWS, n), :].reshape(N_MP * n, BLOCK)
-        sorted_rows = jnp.dot(pick, rows, preferred_element_type=jnp.float32).astype(jnp.bfloat16)
+        ordered = jnp.dot(pick, rows, preferred_element_type=jnp.float32).astype(jnp.bfloat16)
         for k in range(k_rows):
-            flat = lax.dot_general(
-                eye, sorted_rows[k * N_MP : (k + 1) * N_MP], (((1,), (1,)), ((), ())), preferred_element_type=jnp.float32
-            )
-            scale_out[pl.ds(pl.multiple_of(d * ROWS + k * BLOCK, BLOCK), BLOCK), :] = flat.astype(jnp.bfloat16)
-        return 0
-
-    lax.fori_loop(0, N_DP, scales, 0)
+            scale_out[:, pl.ds(d * ROWS + k * BLOCK, BLOCK)] = ordered[k * N_MP : (k + 1) * N_MP]
+
+    pltpu.make_async_copy(rank_hbm, rank_ref, rank_sem).wait()
+    row = lax.broadcasted_iota(jnp.int32, (N_MP, BLOCK), 0)
     lane = lax.broadcasted_iota(jnp.int32, (N_MP, BLOCK), 1)
     total = jnp.zeros((N_MP, BLOCK), jnp.float32)
     for j in range(N_MP):
-        total = total + jnp.where(lane == j, sums[:, rank_ref[j], :], 0.0)
-    check_out[...] = total / (127.0 * math.sqrt(D * BLOCK))
+        total = total + jnp.where(lane == lax.rem(row, 8) * N_MP + j, sums[:, rank_ref[j], :], 0.0)
+    total = total / (127.0 * math.sqrt(D * BLOCK))
+    for p in (0, 1):
+        check_out[pl.ds(p, 1), :] = jnp.sum(total[p * 8 : (p + 1) * 8], axis=0, keepdims=True)
 
     def done(n, _):
         pltpu.make_async_copy(
@@ -288,8 +323,9 @@
 
 def local(weight, rank_map):
     vmem = pl.BlockSpec(memory_space=pltpu.VMEM)
-    smem = pl.BlockSpec(memory_space=pltpu.SMEM)
-    hbm = pl.BlockSpec(memory_space=pl.ANY)
+    hbm = pl.BlockSpec(memory_space=pltpu.HBM)
+    rank_map = pltpu.with_memory_space_constraint(rank_map, pltpu.HBM)
+    weight = pltpu.with_memory_space_constraint(weight, pltpu.HBM)
     dma = pltpu.SemaphoreType.DMA
     land, sums = pl.pallas_call(
         exchange,
@@ -297,15 +333,17 @@
             pltpu.VMEM((N_DP, N_MP, PIECE, BLOCK), jnp.bfloat16),
             pltpu.VMEM((N_MP, N_MP, BLOCK), jnp.float32),
         ),
-        in_specs=[smem, pl.BlockSpec(memory_space=pltpu.HBM)],
+        in_specs=[hbm, hbm],
         out_specs=(vmem, vmem),
         scratch_shapes=[
+            pltpu.SMEM((N_MP,), jnp.int32),
             pltpu.VMEM((N_MP, ROWS, BLOCK), jnp.bfloat16),
             pltpu.VMEM((N_MP, PIECE, BLOCK), jnp.bfloat16),
             pltpu.VMEM((STEPS, PIECE, BLOCK), jnp.bfloat16),
             pltpu.VMEM((N_MP, BLOCK), jnp.float32),
             pltpu.VMEM((N_DP, N_MP, BLOCK), jnp.float32),
             dma(()),
+            dma(()),
             dma((STEPS, 4)),
             dma((STEPS,)),
             dma((3, STEPS, 4)),
@@ -317,21 +355,21 @@
         ],
         compiler_params=pltpu.CompilerParams(collective_id=0, has_side_effects=True, vmem_limit_bytes=12 * MIB),
         name="exchange",
-    )(rank_map, pltpu.with_memory_space_constraint(weight, pltpu.HBM))
+    )(rank_map, weight)
     quant_out, scale_out, check = pl.pallas_call(
         settle,
         out_shape=(
             jax.ShapeDtypeStruct((D, N_MP * BLOCK), jnp.bfloat16),
-            jax.ShapeDtypeStruct((D, N_MP), jnp.bfloat16),
-            jax.ShapeDtypeStruct((N_MP, BLOCK), jnp.float32),
+            jax.ShapeDtypeStruct((N_MP, D), jnp.bfloat16),
+            jax.ShapeDtypeStruct((2, BLOCK), jnp.float32),
         ),
-        in_specs=[smem, vmem, vmem],
+        in_specs=[hbm, vmem, vmem],
         out_specs=(hbm, vmem, vmem),
-        scratch_shapes=[dma(())],
+        scratch_shapes=[pltpu.SMEM((N_MP,), jnp.int32), dma(()), dma(())],
         compiler_params=pltpu.CompilerParams(vmem_limit_bytes=12 * MIB),
         name="settle",
     )(rank_map, land, sums)
-    return quant_out, scale_out, check[:, :N_MP].reshape(N_MP * N_MP)
+    return quant_out, scale_out.T, check.reshape(2 * BLOCK)
 
 
 def solution(mesh):

time: 182 us -> 159 us (0.87)
  Pallas kernels: 178 us -> 157 us
  local copies, waits for them, and re-layouts: 2.34 us -> 0 us
    pallas_call x1, Pallas kernels: 171 us -> 149 us  [local(): pl.pallas_call(exchange, out_shape=(pltpu.VMEM((N_DP, N_MP, PIECE, BLOCK)...]
where the time goes in v3:
time: 159 us; the launch traced here: 157 us
  Pallas kernels  157 us (99%)
    pallas_call x1, Pallas kernels, local(): pl.pallas_call(exchange, out_shape=(pltpu.VMEM((N_DP, N_MP, PIECE, BLOCK)...  149 us
    pallas_call x1, Pallas kernels, local(): pl.pallas_call(settle, out_shape=(jax.ShapeDtypeStruct((D, N_MP * BLOCK),...  7.75 us

profile of v3, /device:TPU:0, one launch (start us, length us, event | category | flops | bytes accessed | tf_op | source)
XLA Modules:
  0.0 157.2 jit_solution(11787924282668069095)
XLA Ops:
  0.6 148.8 %exchange.1 = (bf16[8,16,648,128]{3,2,1,0:T(8,128)(2,1)S(1)}, f32[16,16,128]{2,1,0:T(8,128)S(1)}) custom-call(s32[16]{0:T(128)} %rank_hbm.3, bf16[640,2048]{1,0:T(8,128)(2,1)} %w_hbm.1), custom_call_target="tpu_custom_call" | custom-call | tf_op jit(solution)/shard_map/exchange/pallas_call | solution.py:330
  149.4 7.7 %settle.1 = (bf16[5120,2048]{1,0:T(8,128)(2,1)}, bf16[16,5120]{1,0:T(8,128)(2,1)}, f32[2,128]{1,0:T(2,128)}) custom-call(s32[16]{0:T(128)} %rank_hbm.3, bf16[8,16,648,128]{3,2,1,0:T(8,128)(2,1)S(1)} %get-tuple-element.8.land, f32[16,16,128]{2,1,0:T(8,128)S(1)} %get-tuple-element.9.sums), custom_call_target="tpu_custom_call" | custom-call | tf_op jit(solution)/shard_map/settle/pallas_call | solution.py:359

commit v4 on v3

--- a/solution.py
+++ b/solution.py
@@ -19,6 +19,49 @@
 STEPS = 8
 Z = 4
 MIB = 1024 * 1024
+THIN = (
+    (1, 0, 0),
+    (1, 0, 1),
+    (2, 1, 0),
+    (2, 1, 1),
+    (3, 0, 0),
+    (3, 0, 1),
+    (4, 1, 0),
+    (4, 1, 1),
+)
+PLAIN = (7,)
+EARLY = (
+    ("Y", 2),
+    ("Y", 3),
+    ("R", 1),
+    ("O", 0),
+    ("Y", 4),
+    ("R", 2),
+    ("O", 1),
+    ("C", 0),
+    ("Y", 5),
+    ("R", 3),
+    ("O", 2),
+    ("C", 1),
+    ("Y", 6),
+    ("R", 4),
+    ("O", 3),
+    ("C", 2),
+    ("Y", 7),
+    ("R", 5),
+    ("O", 4),
+    ("C", 3),
+    ("R", 6),
+    ("O", 5),
+    ("C", 4),
+    ("R", 7),
+)
+LATE = (
+    ("O", 6),
+    ("C", 5),
+    ("O", 7),
+    ("C", 6),
+)
 
 
 def exchange(
@@ -97,9 +140,6 @@
 
         lax.fori_loop(0, 4, one, 0)
 
-    def thin(s, way):
-        return jnp.logical_or(s == 1 + way, s == 3 + way)
-
     def piece_copy(src, dst, sem_s, sem_r, dev):
         return pltpu.make_async_remote_copy(src, dst, sem_s, sem_r, device_id=dev, device_id_type=MESH)
 
@@ -117,10 +157,20 @@
     def spread(s, k):
         ref = land.at[lax.rem(k, 2) * Z + z, origin(s, k // 2)]
         for way, dz in ((0, 1), (1, 3)):
-
-            @pl.when(jnp.logical_or(k // 2 == h, jnp.logical_not(thin(s, way))))
-            def _():
-                piece_copy(ref, ref, send.at[s], recvz.at[way, s, k], (h * Z + z_at(dz), mp)).start()
+            send_z = functools.partial(
+                piece_copy, ref, ref, send.at[s], recvz.at[way, s, k], (h * Z + z_at(dz), mp)
+            )
+            thin = [hs for hs in (0, 1) if (s, way, hs) in THIN]
+            if not thin:
+                send_z().start()
+            else:
+                keep = k // 2 == h
+                if len(thin) == 1:
+                    keep = jnp.logical_or(keep, lax.rem(k, 2) != thin[0])
+
+                @pl.when(keep)
+                def _():
+                    send_z().start()
 
     def over_y(s, own=False):
         if not own:
@@ -150,28 +200,27 @@
         block = z_at(2) if way == 2 else (z_at(3) if way == 0 else z_at(1))
         return land.at[lax.rem(k, 2) * Z + block, origin(s, k // 2)]
 
-    def onward(s, rows=(0,)):
-        for row in rows:
+    def onward(s):
+        for row in (0, 1) if s in PLAIN else (0,):
             for way, dz in ((0, 1), (1, 3)):
                 k = lax.rem(h + row, 2) * 2 + way
                 await_recv(recvz.at[way, s, k])
                 ref = arrived(way, s, k)
                 piece_copy(ref, ref, send.at[s], recvz.at[2, s, k], (h * Z + z_at(dz), mp)).start()
+        for way in (0, 1):
+            for hs in (way, 1 - way):
+                if (s, way, hs) in THIN:
+                    if hs != way:
+                        await_recv(recvz.at[way, s, h * 2 + hs])
+                    over(way, s, h * 2 + hs)
 
     def over(way, s, k):
         ref = arrived(way, s, k)
         piece_copy(ref, ref, send.at[s], recvz.at[way, s, k], ((1 - h) * Z + z, mp)).start()
 
-    def cross_near(s):
-        for way in (0, 1):
-
-            @pl.when(thin(s, way))
-            def _():
-                over(way, s, h * 2 + way)
-                await_recv(recvz.at[way, s, h * 2 + 1 - way])
-                over(way, s, h * 2 + 1 - way)
-
     def cross(s):
+        if s in PLAIN:
+            return
         for hs in (0, 1):
             await_recv(recvz.at[2, s, h * 2 + hs])
             over(2, s, h * 2 + hs)
@@ -207,81 +256,47 @@
 
     lax.fori_loop(1, N_DP, give, 0)
 
-    along_y(2)
-    spread_rest(1)
-    onward(0)
-
-    def main(s, _):
-        along_y(s + 1)
-        spread_rest(s)
-        onward(s - 1)
-        cross_near(s - 1)
-        cross(s - 2)
-        return 0
-
-    lax.fori_loop(2, STEPS - 1, main, 0)
-    spread_rest(STEPS - 1)
+    steps = {"Y": along_y, "R": spread_rest, "O": onward, "C": cross}
+    for name, step in EARLY:
+        steps[name](step)
 
     pltpu.make_async_copy(parts.at[pl.ds(0, 7)], parts.at[pl.ds(0, 7)], sem_a).wait()
     whole = jnp.sum(jnp.sum(parts[...], axis=0), axis=1, keepdims=True)
     sums[mp, :, :] = jnp.broadcast_to(whole, (N_MP, BLOCK))
 
-    onward(STEPS - 2)
-    cross(STEPS - 3)
-
     def share(n, _):
         dev = (dp, lax.rem(mp + n, N_MP))
         piece_copy(sums.at[mp], sums.at[mp], send_s, sem_b, dev).start()
         return 0
 
     lax.fori_loop(1, N_MP, share, 0)
-    onward(STEPS - 1, rows=(0, 1))
-    cross(STEPS - 2)
-
-    def finish(s, _):
+    for name, step in LATE:
+        steps[name](step)
+    def sent(sem, n, ref):
+        def one(_, carry):
+            piece_copy(ref, ref, sem, w_sem, (dp, mp)).wait_send()
+            return carry
+
+        lax.fori_loop(0, n, one, 0)
+
+    sent(send_x, 14, staged.at[0])
+    sent(send_s, 7 + 15, part)
+    for step in range(STEPS):
+        sent(send.at[step], 15, staged.at[0])
+    for step in range(STEPS):
         for way in (0, 1):
-
-            @pl.when(jnp.logical_not(thin(s, way)))
-            def _():
-                await_recv(recvz.at[way, s, h * 2 + 1 - way])
-
-            @pl.when(s < STEPS - 1)
-            def _():
-                await_recv(recvz.at[way, s, (1 - h) * 2 + way])
-
-            await_recv(recvz.at[way, s, (1 - h) * 2 + 1 - way])
-            await_recv(recvz.at[2, s, (1 - h) * 2 + way])
-        return 0
-
-    lax.fori_loop(0, STEPS, finish, 0)
-    await_recv(recvz.at[2, STEPS - 1, h * 2])
-    await_recv(recvz.at[2, STEPS - 1, h * 2 + 1])
+            if (step, way, 1 - way) not in THIN:
+                await_recv(recvz.at[way, step, h * 2 + 1 - way])
+            if step not in PLAIN:
+                await_recv(recvz.at[way, step, (1 - h) * 2 + way])
+            else:
+                await_recv(recvz.at[2, step, h * 2 + way])
+            await_recv(recvz.at[way, step, (1 - h) * 2 + 1 - way])
+            await_recv(recvz.at[2, step, (1 - h) * 2 + way])
     pltpu.make_async_copy(sums.at[pl.ds(0, 15)], sums.at[pl.ds(0, 15)], sem_b).wait()
 
-    def sent(s, _):
-        def one(n, _):
-            piece_copy(staged.at[0], staged.at[0], send.at[s], w_sem, (dp, mp)).wait_send()
-            return 0
-
-        lax.fori_loop(0, 15, one, 0)
-        return 0
-
-    lax.fori_loop(0, STEPS, sent, 0)
-
-    def sent_x(n, _):
-        piece_copy(staged.at[0], staged.at[0], send_x, w_sem, (dp, mp)).wait_send()
-        return 0
-
-    lax.fori_loop(0, 14, sent_x, 0)
-
-    def sent_small(n, _):
-        piece_copy(part, part, send_s, w_sem, (dp, mp)).wait_send()
-        return 0
-
-    lax.fori_loop(0, 7 + 15, sent_small, 0)
-
-
-def settle(rank_hbm, land, sums, quant_out, scale_out, check_out, rank_ref, rank_sem, sem):
+
+def settle(rank_hbm, land, sums, quant_out, scale_hbm, check_hbm, rank_ref, scale_out, check_out, rank_sem, sem, sem_s):
     pltpu.make_async_copy(rank_hbm, rank_ref, rank_sem).start()
     for d in range(N_DP):
         for i in range(N_MP):
@@ -312,6 +327,10 @@
     for p in (0, 1):
         check_out[pl.ds(p, 1), :] = jnp.sum(total[p * 8 : (p + 1) * 8], axis=0, keepdims=True)
 
+    small = (pltpu.make_async_copy(scale_out, scale_hbm, sem_s), pltpu.make_async_copy(check_out, check_hbm, rank_sem))
+    for copy in small:
+        copy.start()
+
     def done(n, _):
         pltpu.make_async_copy(
             land.at[0, 0, pl.ds(0, ROWS), :], quant_out.at[pl.ds(0, ROWS), pl.ds(0, BLOCK)], sem
@@ -319,6 +338,8 @@
         return 0
 
     lax.fori_loop(0, N_DP * N_MP, done, 0)
+    for copy in small:
+        copy.wait()
 
 
 def local(weight, rank_map):
@@ -359,13 +380,20 @@
     quant_out, scale_out, check = pl.pallas_call(
         settle,
         out_shape=(
-            jax.ShapeDtypeStruct((D, N_MP * BLOCK), jnp.bfloat16),
-            jax.ShapeDtypeStruct((N_MP, D), jnp.bfloat16),
-            jax.ShapeDtypeStruct((2, BLOCK), jnp.float32),
+            pltpu.HBM((D, N_MP * BLOCK), jnp.bfloat16),
+            pltpu.HBM((N_MP, D), jnp.bfloat16),
+            pltpu.HBM((2, BLOCK), jnp.float32),
         ),
         in_specs=[hbm, vmem, vmem],
-        out_specs=(hbm, vmem, vmem),
-        scratch_shapes=[pltpu.SMEM((N_MP,), jnp.int32), dma(()), dma(())],
+        out_specs=(hbm, hbm, hbm),
+        scratch_shapes=[
+            pltpu.SMEM((N_MP,), jnp.int32),
+            pltpu.VMEM((N_MP, D), jnp.bfloat16),
+            pltpu.VMEM((2, BLOCK), jnp.float32),
+            dma(()),
+            dma(()),
+            dma(()),
+        ],
         compiler_params=pltpu.CompilerParams(vmem_limit_bytes=12 * MIB),
         name="settle",
     )(rank_map, land, sums)

time: 159 us -> 155 us (0.975); the launches traced: 157 us -> 155 us
  Pallas kernels: 157 us -> 154 us
    pallas_call x1, Pallas kernels: 149 us -> 147 us  [local(): pl.pallas_call(exchange, out_shape=(pltpu.VMEM((N_DP, N_MP, PIECE, BLOCK)...]
where the time goes in v4:
time: 155 us
  Pallas kernels  154 us (99%)
    pallas_call x1, Pallas kernels, local(): pl.pallas_call(exchange, out_shape=(pltpu.VMEM((N_DP, N_MP, PIECE, BLOCK)...  147 us
    pallas_call x1, Pallas kernels, local(): pl.pallas_call(settle, out_shape=(pltpu.HBM((D, N_MP * BLOCK), jnp.bfloat...  7.1 us

profile of v4, /device:TPU:0, one launch (start us, length us, event | category | flops | bytes accessed | tf_op | source)
XLA Modules:
  0.0 154.8 jit_solution(2862846272489295568)
XLA Ops:
  0.6 147.1 %exchange.1 = (bf16[8,16,648,128]{3,2,1,0:T(8,128)(2,1)S(1)}, f32[16,16,128]{2,1,0:T(8,128)S(1)}) custom-call(s32[16]{0:T(128)} %rank_hbm.3, bf16[640,2048]{1,0:T(8,128)(2,1)} %w_hbm.1), custom_call_target="tpu_custom_call" | custom-call | tf_op jit(solution)/shard_map/exchange/pallas_call | solution.py:351
  147.7 7.1 %settle.1 = (bf16[5120,2048]{1,0:T(8,128)(2,1)}, bf16[16,5120]{1,0:T(8,128)(2,1)}, f32[2,128]{1,0:T(2,128)}) custom-call(s32[16]{0:T(128)} %rank_hbm.3, bf16[8,16,648,128]{3,2,1,0:T(8,128)(2,1)S(1)} %get-tuple-element.8.land, f32[16,16,128]{2,1,0:T(8,128)S(1)} %get-tuple-element.9.sums), custom_call_target="tpu_custom_call" | custom-call | tf_op jit(solution)/shard_map/settle/pallas_call | solution.py:380

commit v5 on v4

--- a/solution.py
+++ b/solution.py
@@ -27,13 +27,12 @@
     (3, 0, 0),
     (3, 0, 1),
     (4, 1, 0),
-    (4, 1, 1),
 )
 PLAIN = (7,)
 EARLY = (
     ("Y", 2),
+    ("R", 1),
     ("Y", 3),
-    ("R", 1),
     ("O", 0),
     ("Y", 4),
     ("R", 2),
@@ -54,13 +53,13 @@
     ("R", 6),
     ("O", 5),
     ("C", 4),
+    ("O", 6),
+    ("C", 5),
     ("R", 7),
 )
 LATE = (
-    ("O", 6),
-    ("C", 5),
+    ("C", 6),
     ("O", 7),
-    ("C", 6),
 )
 
 

time: 155 us -> 153 us (0.987)
  no operation moved by 1% of the time
where the time goes in v5:
time: 153 us
  Pallas kernels  153 us (100%)
    pallas_call x1, Pallas kernels, local(): pl.pallas_call(exchange, out_shape=(pltpu.VMEM((N_DP, N_MP, PIECE, BLOCK)...  146 us
    pallas_call x1, Pallas kernels, local(): pl.pallas_call(settle, out_shape=(pltpu.HBM((D, N_MP * BLOCK), jnp.bfloat...  7.1 us

profile of v5, /device:TPU:0, one launch (start us, length us, event | category | flops | bytes accessed | tf_op | source)
XLA Modules:
  0.0 153.3 jit_solution(191493069026837258)
XLA Ops:
  0.6 145.5 %exchange.1 = (bf16[8,16,648,128]{3,2,1,0:T(8,128)(2,1)S(1)}, f32[16,16,128]{2,1,0:T(8,128)S(1)}) custom-call(s32[16]{0:T(128)} %rank_hbm.3, bf16[640,2048]{1,0:T(8,128)(2,1)} %w_hbm.1), custom_call_target="tpu_custom_call" | custom-call | tf_op jit(solution)/shard_map/exchange/pallas_call | solution.py:350
  146.2 7.1 %settle.1 = (bf16[5120,2048]{1,0:T(8,128)(2,1)}, bf16[16,5120]{1,0:T(8,128)(2,1)}, f32[2,128]{1,0:T(2,128)}) custom-call(s32[16]{0:T(128)} %rank_hbm.3, bf16[8,16,648,128]{3,2,1,0:T(8,128)(2,1)S(1)} %get-tuple-element.8.land, f32[16,16,128]{2,1,0:T(8,128)S(1)} %get-tuple-element.9.sums), custom_call_target="tpu_custom_call" | custom-call | tf_op jit(solution)/shard_map/settle/pallas_call | solution.py:379

commit v6 on v5

--- a/solution.py
+++ b/solution.py
@@ -28,6 +28,8 @@
     (3, 0, 1),
     (4, 1, 0),
 )
+HALF = ((4, 1, 1), )
+CUT = 328
 PLAIN = (7,)
 EARLY = (
     ("Y", 2),
@@ -160,7 +162,24 @@
                 piece_copy, ref, ref, send.at[s], recvz.at[way, s, k], (h * Z + z_at(dz), mp)
             )
             thin = [hs for hs in (0, 1) if (s, way, hs) in THIN]
-            if not thin:
+            half = [hs for hs in (0, 1) if (s, way, hs) in HALF]
+            if half:
+                whole = jnp.logical_or(k // 2 == h, lax.rem(k, 2) != half[0])
+
+                full = whole
+                if thin:
+                    full = jnp.logical_or(k // 2 == h, jnp.logical_and(whole, lax.rem(k, 2) != thin[0]))
+
+                @pl.when(full)
+                def _():
+                    send_z().start()
+
+                @pl.when(jnp.logical_not(whole))
+                def _():
+                    top = ref.at[pl.ds(0, CUT), :]
+                    piece_copy(top, top, send.at[s], recvz.at[way, s, k], (h * Z + z_at(dz), mp)).start()
+
+            elif not thin:
                 send_z().start()
             else:
                 keep = k // 2 == h
@@ -175,8 +194,8 @@
         if not own:
             await_recv(recv1.at[s, home])
         ref = land.at[dp, origin(s, yl)]
+        spread(s, home)
         piece_copy(ref, ref, send.at[s], recv1.at[s, home], ((1 - h) * Z + z, mp)).start()
-        spread(s, home)
 
     def beside_y(s, own=False):
         if not own:
@@ -208,13 +227,15 @@
                 piece_copy(ref, ref, send.at[s], recvz.at[2, s, k], (h * Z + z_at(dz), mp)).start()
         for way in (0, 1):
             for hs in (way, 1 - way):
-                if (s, way, hs) in THIN:
+                if (s, way, hs) in THIN or (s, way, hs) in HALF:
                     if hs != way:
                         await_recv(recvz.at[way, s, h * 2 + hs])
-                    over(way, s, h * 2 + hs)
-
-    def over(way, s, k):
+                    over(way, s, h * 2 + hs, (s, way, hs) in HALF)
+
+    def over(way, s, k, rest=False):
         ref = arrived(way, s, k)
+        if rest:
+            ref = ref.at[pl.ds(CUT, PIECE - CUT), :]
         piece_copy(ref, ref, send.at[s], recvz.at[way, s, k], ((1 - h) * Z + z, mp)).start()
 
     def cross(s):
@@ -284,7 +305,7 @@
         sent(send.at[step], 15, staged.at[0])
     for step in range(STEPS):
         for way in (0, 1):
-            if (step, way, 1 - way) not in THIN:
+            if (step, way, 1 - way) not in THIN + HALF:
                 await_recv(recvz.at[way, step, h * 2 + 1 - way])
             if step not in PLAIN:
                 await_recv(recvz.at[way, step, (1 - h) * 2 + way])

time: 153 us -> 153 us (level)
  no operation moved by 1% of the time
where the time goes in v6:
time: 153 us
  Pallas kernels  152 us (99%)
    pallas_call x1, Pallas kernels, local(): pl.pallas_call(exchange, out_shape=(pltpu.VMEM((N_DP, N_MP, PIECE, BLOCK)...  145 us
    pallas_call x1, Pallas kernels, local(): pl.pallas_call(settle, out_shape=(pltpu.HBM((D, N_MP * BLOCK), jnp.bfloat...  7.1 us

profile of v6, /device:TPU:0, one launch (start us, length us, event | category | flops | bytes accessed | tf_op | source)
XLA Modules:
  0.0 153.0 jit_solution(7470292294296160033)
XLA Ops:
  0.6 145.3 %exchange.1 = (bf16[8,16,648,128]{3,2,1,0:T(8,128)(2,1)S(1)}, f32[16,16,128]{2,1,0:T(8,128)S(1)}) custom-call(s32[16]{0:T(128)} %rank_hbm.3, bf16[640,2048]{1,0:T(8,128)(2,1)} %w_hbm.1), custom_call_target="tpu_custom_call" | custom-call | tf_op jit(solution)/shard_map/exchange/pallas_call | solution.py:371
  145.9 7.1 %settle.1 = (bf16[5120,2048]{1,0:T(8,128)(2,1)}, bf16[16,5120]{1,0:T(8,128)(2,1)}, f32[2,128]{1,0:T(2,128)}) custom-call(s32[16]{0:T(128)} %rank_hbm.3, bf16[8,16,648,128]{3,2,1,0:T(8,128)(2,1)S(1)} %get-tuple-element.8.land, f32[16,16,128]{2,1,0:T(8,128)S(1)} %get-tuple-element.9.sums), custom_call_target="tpu_custom_call" | custom-call | tf_op jit(solution)/shard_map/settle/pallas_call | solution.py:400

commit v7 on v5

--- a/solution.py
+++ b/solution.py
@@ -47,6 +47,8 @@
     ("O", 3),
     ("C", 2),
     ("Y", 7),
+)
+LATE = (
     ("R", 5),
     ("O", 4),
     ("C", 3),
@@ -56,8 +58,6 @@
     ("O", 6),
     ("C", 5),
     ("R", 7),
-)
-LATE = (
     ("C", 6),
     ("O", 7),
 )

time: 153 us -> 153 us (level)
  no operation moved by 1% of the time
where the time goes in v7:
time: 153 us
  Pallas kernels  153 us (100%)
    pallas_call x1, Pallas kernels, local(): pl.pallas_call(exchange, out_shape=(pltpu.VMEM((N_DP, N_MP, PIECE, BLOCK)...  146 us
    pallas_call x1, Pallas kernels, local(): pl.pallas_call(settle, out_shape=(pltpu.HBM((D, N_MP * BLOCK), jnp.bfloat...  7.1 us

profile of v7, /device:TPU:0, one launch (start us, length us, event | category | flops | bytes accessed | tf_op | source)
XLA Modules:
  0.0 153.3 jit_solution(9556943146959907847)
XLA Ops:
  0.6 145.5 %exchange.1 = (bf16[8,16,648,128]{3,2,1,0:T(8,128)(2,1)S(1)}, f32[16,16,128]{2,1,0:T(8,128)S(1)}) custom-call(s32[16]{0:T(128)} %rank_hbm.3, bf16[640,2048]{1,0:T(8,128)(2,1)} %w_hbm.1), custom_call_target="tpu_custom_call" | custom-call | tf_op jit(solution)/shard_map/exchange/pallas_call | solution.py:350
  146.2 7.1 %settle.1 = (bf16[5120,2048]{1,0:T(8,128)(2,1)}, bf16[16,5120]{1,0:T(8,128)(2,1)}, f32[2,128]{1,0:T(2,128)}) custom-call(s32[16]{0:T(128)} %rank_hbm.3, bf16[8,16,648,128]{3,2,1,0:T(8,128)(2,1)S(1)} %get-tuple-element.8.land, f32[16,16,128]{2,1,0:T(8,128)S(1)} %get-tuple-element.9.sums), custom_call_target="tpu_custom_call" | custom-call | tf_op jit(solution)/shard_map/settle/pallas_call | solution.py:379
